TPU v7x, 256 devices: a whole 4x4x8 slice. The times are simulated.
256 devices in a mesh: gx: 8 (over y, core), gy: 32 (over x, z).
Axes of the slice: x: 4, y: 4, z: 8, core: 2. Of those that a mesh axis runs over, the one named last changes fastest.
Arguments:
- source: float32 [64, 32, 4096], P(None, 'gx', 'gy'), may hold values from -6 to 6
- initial: float32 [64, 32, 4096], P(None, 'gx', 'gy'), may hold values from -6 to 6
- reaction: float32 [64, 32, 4096], P(None, 'gx', 'gy'), may hold values from 1 to 3
- stiffness: float32 [32, 4096], P('gx', 'gy'), may hold values from 0.5 to 2
- line_op: float32 [8, 8], replicated, may hold values from -1.6 to 5.6
- face_deriv: float32 [8], replicated, may hold values from -2 to 2
- wall_flags: int32 [4, 32, 4096], P(None, 'gx', 'gy'), may hold values 0 or 1
Outputs:
- hessenberg: float32 [6, 5], replicated
- krylov_basis: float32 [6, 64, 32, 4096], P(None, None, 'gx', 'gy')
All inputs are finite; a program needn't handle non-finite values. No bound on the sum of `wall_flags` on one device may be relied on, other than what follows from the above.
Results may differ from a plain program's by a relative error of at most 0.0003.
Values sent between devices are 32-bit elements; how exact they have to be, the bound alone decides.
No kernel may reach another device: no remote copies, remote signals or barrier semaphores. Data moves between devices by JAX's collectives and lax.ppermute only.
A program may use at most 64 MiB of HBM per device.

v0:
```python
import jax
import jax.numpy as jnp
from jax import lax
from jax.sharding import Mesh
from jax.sharding import PartitionSpec as P

P_SIZE = 8
ITERS = 5
GX = ("gx_0", "gx_1")
GY = ("gy_0", "gy_1")


TAU = 2.0
FLOOR = 0.1


def extended(array, sides, width):
    for axis, dim in sides:
        devices, length = (lax.axis_size(axis), array.shape[dim])
        up = [(i, (i + 1) % devices) for i in range(devices)]
        down = [(j, i) for i, j in up]
        last = lax.slice_in_dim(array, length - width, length, axis=dim)
        leading = lax.slice_in_dim(array, 0, width, axis=dim)
        before = lax.ppermute(last, axis, up)
        after = lax.ppermute(leading, axis, down)
        array = jnp.concatenate([before, array, after], axis=dim)
    return array


def sent_to_all(array, axis):
    copies = jnp.broadcast_to(array, (lax.axis_size(axis), *array.shape))
    return lax.all_to_all(copies, axis, split_axis=0, concat_axis=0, tiled=True)


def over_copies(array, axis):
    everything = sent_to_all(array, axis)
    return jnp.sum(everything, axis=0)


def by_axis(array, axes):
    far, near = axes
    nearer = over_copies(array, near)
    return over_copies(nearer, far)


def together(arrays, axis):
    vector, at, gathered = (jnp.concatenate([a.reshape(-1) for a in arrays]), 0, [])
    subtotal = by_axis(vector, axis)
    for a in arrays:
        gathered.append(subtotal[at : at + a.size].reshape(a.shape))
        at += a.size
    return tuple(gathered)


def local_total(values):
    return jnp.sum(jnp.sum(values, axis=0))


def x_traces(nodes, face_deriv):
    highest = lax.Precision.HIGHEST
    lower = jnp.einsum("c,cbxy->bxy", face_deriv, nodes, precision=highest)
    upper = jnp.einsum("c,cbxy->bxy", face_deriv[::-1], nodes, precision=highest)
    return jnp.stack([nodes[0], lower, nodes[-1], upper])


def y_traces(nodes, face_deriv):
    highest = lax.Precision.HIGHEST
    lower = jnp.einsum("c,acxy->axy", face_deriv, nodes, precision=highest)
    upper = jnp.einsum("c,acxy->axy", face_deriv[::-1], nodes, precision=highest)
    return jnp.stack([nodes[:, 0], lower, nodes[:, -1], upper])


def apply_op(field, reaction, stiffness, line_op, face_deriv, opened):
    highest = lax.Precision.HIGHEST
    nodes = field.reshape(P_SIZE, P_SIZE, field.shape[1], field.shape[2])
    interior = stiffness * (
        jnp.einsum("ac,cbxy->abxy", line_op, nodes, precision=highest)
        + jnp.einsum("bc,acxy->abxy", line_op, nodes, precision=highest)
    )
    xside = extended(x_traces(nodes, face_deriv), ((GX, 2),), 1)
    yside = extended(y_traces(nodes, face_deriv), ((GY, 3),), 1)
    x_own = xside[:, :, 1:-1]
    y_own = yside[:, :, :, 1:-1]
    east_nb = xside[0:2, :, 2:]
    west_nb = xside[2:4, :, :-2]
    north_nb = yside[0:2, :, :, 2:]
    south_nb = yside[2:4, :, :, :-2]
    add_east = TAU * (x_own[2] - opened[1] * east_nb[0]) + 0.5 * (x_own[3] - opened[1] * east_nb[1])
    add_west = TAU * (x_own[0] - opened[0] * west_nb[0]) + 0.5 * (x_own[1] - opened[0] * west_nb[1])
    add_north = TAU * (y_own[2] - opened[3] * north_nb[0]) + 0.5 * (
        y_own[3] - opened[3] * north_nb[1]
    )
    add_south = TAU * (y_own[0] - opened[2] * south_nb[0]) + 0.5 * (
        y_own[1] - opened[2] * south_nb[1]
    )
    result = reaction.reshape(nodes.shape) * nodes + interior
    result = result.at[0].add(add_west).at[P_SIZE - 1].add(add_east)
    result = result.at[:, 0].add(add_south).at[:, P_SIZE - 1].add(add_north)
    return result.reshape(field.shape)


def norm_scale(vector, total):
    squares = by_axis(local_total(vector * vector), (("gx_0", "gx_1"), ("gy_0", "gy_1")))
    return jnp.sqrt(squares / total + FLOOR)


def body(source, initial, reaction, stiffness, line_op, face_deriv, wall_flags):
    highest = lax.Precision.HIGHEST
    total = float(
        P_SIZE * P_SIZE * source.shape[1] * lax.axis_size(GX) * source.shape[2] * lax.axis_size(GY)
    )
    opened = 1.0 - wall_flags.astype(jnp.float32)

    def operate(field):
        return apply_op(field, reaction, stiffness, line_op, face_deriv, opened)

    def products(basis, image):
        per_cell = jnp.einsum("kqxy,qxy->kxy", basis, image, precision=highest)
        return jnp.sum(per_cell, axis=(1, 2))

    first = source - operate(initial)
    basis = jnp.zeros((ITERS + 1,) + source.shape, jnp.float32)
    hessen = jnp.zeros((ITERS + 1, ITERS), jnp.float32)
    rows = lax.broadcasted_iota(jnp.int32, (ITERS + 1, ITERS), 0)
    cols = lax.broadcasted_iota(jnp.int32, (ITERS + 1, ITERS), 1)
    slots = lax.broadcasted_iota(jnp.int32, (ITERS + 1,), 0)

    def advance(step, carry):
        basis, hessen, pending = carry
        image = operate(pending)
        local = products(basis, image)
        projected, crossed, squares = together(
            (local, local_total(pending * image), local_total(pending * pending)),
            (("gx_0", "gx_1"), ("gy_0", "gy_1")),
        )
        beta = jnp.sqrt(squares / total + FLOOR)
        basis = lax.dynamic_update_index_in_dim(basis, pending / beta, step, 0)
        coeffs = projected / (total * beta) + jnp.where(
            slots == step, crossed / (total * beta * beta), 0.0
        )
        pending = image / beta - jnp.einsum("k,kqxy->qxy", coeffs, basis, precision=highest)
        hessen = hessen + jnp.where(cols == step, coeffs[:, None], 0.0)
        hessen = hessen + jnp.where((rows == step) & (cols == step - 1), beta, 0.0)
        return (basis, hessen, pending)

    basis, hessen, pending = lax.fori_loop(0, ITERS, advance, (basis, hessen, first))
    beta = norm_scale(pending, total)
    basis = basis.at[ITERS].set(pending / beta)
    hessen = hessen + jnp.where((rows == ITERS) & (cols == ITERS - 1), beta, 0.0)
    return (hessen, basis)


def solution(mesh):
    finer = Mesh(mesh.devices.reshape(4, 2, 4, 8), ("gx_0", "gx_1", "gy_0", "gy_1"))
    placed = (
        P(None, GX, GY),
        P(None, GX, GY),
        P(None, GX, GY),
        P(GX, GY),
        P(),
        P(),
        P(None, GX, GY),
    )
    return jax.shard_map(
        body, mesh=finer, in_specs=placed, out_specs=(P(), P(None, None, GX, GY)), check_vma=False
    )
```

profile of v0, /device:TPU:1, one launch (start us, length us, event | category | flops | bytes accessed | tf_op | source)
XLA Modules:
  0.0 283.4 jit_solution(14238751675292075828)
XLA Ops:
  2.2 2.7 collective-permute-start.4
  7.3 6.2 %collective-permute-start.7 = (f32[4,8,4,1]{3,1,2,0:T(8,128)S(1)}, f32[4,8,4,1]{3,1,2,0:T(8,128)S(1)}, u32[]{:S(2)}, u32[]{:S(2)}) collective-permute-start(f32[4,8,4,1]{3,1,2,0:T(8,128)S(1)} %get-tuple-element.670), channel_id=1, source_target_pairs={{1,0},{2,1},{3,2},{4,3},{5,4},{6,5},{7,6},{8,7},{9,8},{10,9},{11,1... | collective-permute-start | bytes 1544 | tf_op jit(solution)/shard_map/ppermute | solution.py:25
  17.0 239.6 %while.31 = (s32[]{:T(128)}, f32[6,64,4,128]{3,1,2,0:T(8,128)S(1)}, f32[6,5]{1,0:T(8,128)S(1)}, f32[64,4,128]{2,0,1:T(8,128)S(1)}, f32[64,4,128]{2,0,1:T(8,128)S...) while((s32[]{:T(128)}, f32[6,64,4,128]{3,1,2,0:T(8,128)S(1)}, ...), condition=%wide.region_5.6_spmd.clone.clone, body=%wide.region_0.5_spmd.clone.clone.sunk | while | flops 13279853 | bytes 6174235 | solution.py:146
  17.7 2.5 collective-permute-start
  21.0 4.8 %collective-permute-start.3 = (f32[4,8,4,1]{3,1,2,0:T(8,128)S(1)}, f32[4,8,4,1]{3,1,2,0:T(8,128)S(1)}, u32[]{:S(2)}, u32[]{:S(2)}) collective-permute-start(f32[4,8,4,1]{3,1,2,0:T(8,128)S(1)} %get-tuple-element.765), channel_id=1, source_target_pairs={{1,0},{2,1},{3,2},{4,3},{5,4},{6,5},{7,6},{8,7},{9,8},{10,9},{11,1... | collective-permute-start | bytes 1544 | tf_op jit(solution)/shard_map/while/body/eval_jaxpr/ppermute | solution.py:25
  28.3 2.6 convolution_bitcast_fusion.2
  31.0 1.4 pad_maximum_fusion.48
  33.0 6.4 %all-to-all-start = ((f32[32,1,8]{2,1,0:T(1,128)}), f32[32,1,8]{2,1,0:T(1,128)S(1)}, u32[]{:S(2)}, u32[]{:S(2)}) async-start(f32[32,1,8]{2,1,0:T(1,128)} %broadcast_in_dim.147), calls=%async_computation | async-start | bytes 32768 | tf_op jit(solution)/shard_map/while/body/eval_jaxpr/all_to_all | solution.py:32
  39.4 8.6 %all-to-all-done = f32[32,1,8]{2,1,0:T(1,128)S(1)} async-done(((f32[32,1,8]{2,1,0:T(1,128)}), f32[32,1,8]{2,1,0:T(1,128)S(1)}, u32[]{:S(2)}, u32[]{:S(2)}) %all-to-all-start) | async-done | bytes 1056 | tf_op jit(solution)/shard_map/while/body/eval_jaxpr/all_to_all | solution.py:32
  48.6 9.0 %all-to-all-start.1 = ((f32[8,1,8]{2,1,0:T(1,128)}), f32[8,1,8]{2,1,0:T(1,128)S(1)}, u32[]{:S(2)}, u32[]{:S(2)}) async-start(f32[8,1,8]{2,1,0:T(1,128)} %broadcast_in_dim.148), calls=%async_computation.1 | async-start | bytes 8192 | tf_op jit(solution)/shard_map/while/body/eval_jaxpr/all_to_all | solution.py:32
  57.6 4.5 %all-to-all-done.1 = f32[8,1,8]{2,1,0:T(1,128)S(1)} async-done(((f32[8,1,8]{2,1,0:T(1,128)}), f32[8,1,8]{2,1,0:T(1,128)S(1)}, u32[]{:S(2)}, u32[]{:S(2)}) %all-to-all-start.1) | async-done | bytes 288 | tf_op jit(solution)/shard_map/while/body/eval_jaxpr/all_to_all | solution.py:32
  64.1 1.5 fusion.211
  69.0 4.5 %collective-permute-start.3 = (f32[4,8,4,1]{3,1,2,0:T(8,128)S(1)}, f32[4,8,4,1]{3,1,2,0:T(8,128)S(1)}, u32[]{:S(2)}, u32[]{:S(2)}) collective-permute-start(f32[4,8,4,1]{3,1,2,0:T(8,128)S(1)} %get-tuple-element.765), channel_id=1, source_target_pairs={{1,0},{2,1},{3,2},{4,3},{5,4},{6,5},{7,6},{8,7},{9,8},{10,9},{11,1... | collective-permute-start | bytes 1544 | tf_op jit(solution)/shard_map/while/body/eval_jaxpr/ppermute | solution.py:25
  76.1 2.6 convolution_bitcast_fusion.2
  78.7 1.4 pad_maximum_fusion.48
  80.7 6.4 %all-to-all-start = ((f32[32,1,8]{2,1,0:T(1,128)}), f32[32,1,8]{2,1,0:T(1,128)S(1)}, u32[]{:S(2)}, u32[]{:S(2)}) async-start(f32[32,1,8]{2,1,0:T(1,128)} %broadcast_in_dim.147), calls=%async_computation | async-start | bytes 32768 | tf_op jit(solution)/shard_map/while/body/eval_jaxpr/all_to_all | solution.py:32
  87.1 8.6 %all-to-all-done = f32[32,1,8]{2,1,0:T(1,128)S(1)} async-done(((f32[32,1,8]{2,1,0:T(1,128)}), f32[32,1,8]{2,1,0:T(1,128)S(1)}, u32[]{:S(2)}, u32[]{:S(2)}) %all-to-all-start) | async-done | bytes 1056 | tf_op jit(solution)/shard_map/while/body/eval_jaxpr/all_to_all | solution.py:32
  96.3 8.8 %all-to-all-start.1 = ((f32[8,1,8]{2,1,0:T(1,128)}), f32[8,1,8]{2,1,0:T(1,128)S(1)}, u32[]{:S(2)}, u32[]{:S(2)}) async-start(f32[8,1,8]{2,1,0:T(1,128)} %broadcast_in_dim.148), calls=%async_computation.1 | async-start | bytes 8192 | tf_op jit(solution)/shard_map/while/body/eval_jaxpr/all_to_all | solution.py:32
  105.2 4.5 %all-to-all-done.1 = f32[8,1,8]{2,1,0:T(1,128)S(1)} async-done(((f32[8,1,8]{2,1,0:T(1,128)}), f32[8,1,8]{2,1,0:T(1,128)S(1)}, u32[]{:S(2)}, u32[]{:S(2)}) %all-to-all-start.1) | async-done | bytes 288 | tf_op jit(solution)/shard_map/while/body/eval_jaxpr/all_to_all | solution.py:32
  111.7 1.5 fusion.211
  116.6 4.5 %collective-permute-start.3 = (f32[4,8,4,1]{3,1,2,0:T(8,128)S(1)}, f32[4,8,4,1]{3,1,2,0:T(8,128)S(1)}, u32[]{:S(2)}, u32[]{:S(2)}) collective-permute-start(f32[4,8,4,1]{3,1,2,0:T(8,128)S(1)} %get-tuple-element.765), channel_id=1, source_target_pairs={{1,0},{2,1},{3,2},{4,3},{5,4},{6,5},{7,6},{8,7},{9,8},{10,9},{11,1... | collective-permute-start | bytes 1544 | tf_op jit(solution)/shard_map/while/body/eval_jaxpr/ppermute | solution.py:25
  123.6 2.6 convolution_bitcast_fusion.2
  126.3 1.4 pad_maximum_fusion.48
  128.3 6.4 %all-to-all-start = ((f32[32,1,8]{2,1,0:T(1,128)}), f32[32,1,8]{2,1,0:T(1,128)S(1)}, u32[]{:S(2)}, u32[]{:S(2)}) async-start(f32[32,1,8]{2,1,0:T(1,128)} %broadcast_in_dim.147), calls=%async_computation | async-start | bytes 32768 | tf_op jit(solution)/shard_map/while/body/eval_jaxpr/all_to_all | solution.py:32
  134.7 8.6 %all-to-all-done = f32[32,1,8]{2,1,0:T(1,128)S(1)} async-done(((f32[32,1,8]{2,1,0:T(1,128)}), f32[32,1,8]{2,1,0:T(1,128)S(1)}, u32[]{:S(2)}, u32[]{:S(2)}) %all-to-all-start) | async-done | bytes 1056 | tf_op jit(solution)/shard_map/while/body/eval_jaxpr/all_to_all | solution.py:32
  143.9 8.8 %all-to-all-start.1 = ((f32[8,1,8]{2,1,0:T(1,128)}), f32[8,1,8]{2,1,0:T(1,128)S(1)}, u32[]{:S(2)}, u32[]{:S(2)}) async-start(f32[8,1,8]{2,1,0:T(1,128)} %broadcast_in_dim.148), calls=%async_computation.1 | async-start | bytes 8192 | tf_op jit(solution)/shard_map/while/body/eval_jaxpr/all_to_all | solution.py:32
  152.7 4.5 %all-to-all-done.1 = f32[8,1,8]{2,1,0:T(1,128)S(1)} async-done(((f32[8,1,8]{2,1,0:T(1,128)}), f32[8,1,8]{2,1,0:T(1,128)S(1)}, u32[]{:S(2)}, u32[]{:S(2)}) %all-to-all-start.1) | async-done | bytes 288 | tf_op jit(solution)/shard_map/while/body/eval_jaxpr/all_to_all | solution.py:32
  159.3 1.5 fusion.211
  164.2 4.5 %collective-permute-start.3 = (f32[4,8,4,1]{3,1,2,0:T(8,128)S(1)}, f32[4,8,4,1]{3,1,2,0:T(8,128)S(1)}, u32[]{:S(2)}, u32[]{:S(2)}) collective-permute-start(f32[4,8,4,1]{3,1,2,0:T(8,128)S(1)} %get-tuple-element.765), channel_id=1, source_target_pairs={{1,0},{2,1},{3,2},{4,3},{5,4},{6,5},{7,6},{8,7},{9,8},{10,9},{11,1... | collective-permute-start | bytes 1544 | tf_op jit(solution)/shard_map/while/body/eval_jaxpr/ppermute | solution.py:25
  171.2 2.6 convolution_bitcast_fusion.2
  173.9 1.4 pad_maximum_fusion.48
  175.9 6.4 %all-to-all-start = ((f32[32,1,8]{2,1,0:T(1,128)}), f32[32,1,8]{2,1,0:T(1,128)S(1)}, u32[]{:S(2)}, u32[]{:S(2)}) async-start(f32[32,1,8]{2,1,0:T(1,128)} %broadcast_in_dim.147), calls=%async_computation | async-start | bytes 32768 | tf_op jit(solution)/shard_map/while/body/eval_jaxpr/all_to_all | solution.py:32
  182.2 8.6 %all-to-all-done = f32[32,1,8]{2,1,0:T(1,128)S(1)} async-done(((f32[32,1,8]{2,1,0:T(1,128)}), f32[32,1,8]{2,1,0:T(1,128)S(1)}, u32[]{:S(2)}, u32[]{:S(2)}) %all-to-all-start) | async-done | bytes 1056 | tf_op jit(solution)/shard_map/while/body/eval_jaxpr/all_to_all | solution.py:32
  191.5 8.8 %all-to-all-start.1 = ((f32[8,1,8]{2,1,0:T(1,128)}), f32[8,1,8]{2,1,0:T(1,128)S(1)}, u32[]{:S(2)}, u32[]{:S(2)}) async-start(f32[8,1,8]{2,1,0:T(1,128)} %broadcast_in_dim.148), calls=%async_computation.1 | async-start | bytes 8192 | tf_op jit(solution)/shard_map/while/body/eval_jaxpr/all_to_all | solution.py:32
  200.3 4.5 %all-to-all-done.1 = f32[8,1,8]{2,1,0:T(1,128)S(1)} async-done(((f32[8,1,8]{2,1,0:T(1,128)}), f32[8,1,8]{2,1,0:T(1,128)S(1)}, u32[]{:S(2)}, u32[]{:S(2)}) %all-to-all-start.1) | async-done | bytes 288 | tf_op jit(solution)/shard_map/while/body/eval_jaxpr/all_to_all | solution.py:32
  206.9 1.5 fusion.211
  211.7 4.5 %collective-permute-start.3 = (f32[4,8,4,1]{3,1,2,0:T(8,128)S(1)}, f32[4,8,4,1]{3,1,2,0:T(8,128)S(1)}, u32[]{:S(2)}, u32[]{:S(2)}) collective-permute-start(f32[4,8,4,1]{3,1,2,0:T(8,128)S(1)} %get-tuple-element.765), channel_id=1, source_target_pairs={{1,0},{2,1},{3,2},{4,3},{5,4},{6,5},{7,6},{8,7},{9,8},{10,9},{11,1... | collective-permute-start | bytes 1544 | tf_op jit(solution)/shard_map/while/body/eval_jaxpr/ppermute | solution.py:25
  218.8 2.6 convolution_bitcast_fusion.2
  221.4 1.4 pad_maximum_fusion.48
  223.4 6.4 %all-to-all-start = ((f32[32,1,8]{2,1,0:T(1,128)}), f32[32,1,8]{2,1,0:T(1,128)S(1)}, u32[]{:S(2)}, u32[]{:S(2)}) async-start(f32[32,1,8]{2,1,0:T(1,128)} %broadcast_in_dim.147), calls=%async_computation | async-start | bytes 32768 | tf_op jit(solution)/shard_map/while/body/eval_jaxpr/all_to_all | solution.py:32
  229.8 8.6 %all-to-all-done = f32[32,1,8]{2,1,0:T(1,128)S(1)} async-done(((f32[32,1,8]{2,1,0:T(1,128)}), f32[32,1,8]{2,1,0:T(1,128)S(1)}, u32[]{:S(2)}, u32[]{:S(2)}) %all-to-all-start) | async-done | bytes 1056 | tf_op jit(solution)/shard_map/while/body/eval_jaxpr/all_to_all | solution.py:32
  239.0 8.8 %all-to-all-start.1 = ((f32[8,1,8]{2,1,0:T(1,128)}), f32[8,1,8]{2,1,0:T(1,128)S(1)}, u32[]{:S(2)}, u32[]{:S(2)}) async-start(f32[8,1,8]{2,1,0:T(1,128)} %broadcast_in_dim.148), calls=%async_computation.1 | async-start | bytes 8192 | tf_op jit(solution)/shard_map/while/body/eval_jaxpr/all_to_all | solution.py:32
  247.9 4.5 %all-to-all-done.1 = f32[8,1,8]{2,1,0:T(1,128)S(1)} async-done(((f32[8,1,8]{2,1,0:T(1,128)}), f32[8,1,8]{2,1,0:T(1,128)S(1)}, u32[]{:S(2)}, u32[]{:S(2)}) %all-to-all-start.1) | async-done | bytes 288 | tf_op jit(solution)/shard_map/while/body/eval_jaxpr/all_to_all | solution.py:32
  254.4 1.5 fusion.211
  257.3 1.3 broadcast_in_dim.113
  258.6 3.8 %all-to-all-start.2 = ((f32[32,1,1]{2,1,0:T(1,128)}), f32[32,1,1]{2,1,0:T(1,128)S(1)}, u32[]{:S(2)}, u32[]{:S(2)}) async-start(f32[32,1,1]{2,1,0:T(1,128)} %broadcast_in_dim.113), calls=%async_computation.2 | async-start | bytes 32768 | tf_op jit(solution)/shard_map/all_to_all | solution.py:32
  262.9 8.1 %all-to-all-done.2 = f32[32,1,1]{2,1,0:T(1,128)S(1)} async-done(((f32[32,1,1]{2,1,0:T(1,128)}), f32[32,1,1]{2,1,0:T(1,128)S(1)}, u32[]{:S(2)}, u32[]{:S(2)}) %all-to-all-start.2) | async-done | bytes 160 | tf_op jit(solution)/shard_map/all_to_all | solution.py:32
  272.3 8.8 %all_to_all.46 = f32[8,1,1]{2,1,0:T(1,128)S(1)} all-to-all(f32[8,1,1]{2,1,0:T(1,128)S(1)} %broadcast_in_dim.114), channel_id=1, replica_groups=mesh['gx_0'=4,'gx_1'=2,'gy_0'=4,'gy_1'=8] {'gx_0','gx_1'}, dimensions={0} | all-to-all | bytes 64 | tf_op jit(solution)/shard_map/all_to_all | solution.py:32
  (293 shorter events, 48.4 us)
Async XLA Ops:
  0.6 0.9 copy-start.5
  2.2 12.7 %collective-permute-start.4 = (f32[4,8,1,128]{3,1,2,0:T(8,128)S(1)}, f32[4,8,1,128]{3,1,2,0:T(8,128)S(1)}, u32[]{:S(2)}, u32[]{:S(2)}) collective-permute-start(f32[4,8,1,128]{3,1,2,0:T(8,128)S(1)} %get-tuple-element.673), channel_id=1, source_target_pairs={{0,32},{32,64},{64,96},{96,128},{128,160},{160,192},{192,224},{224... | collective-permute-start | bytes 49160 | tf_op jit(solution)/shard_map/ppermute | solution.py:24
  4.9 10.2 %collective-permute-start.5 = (f32[4,8,1,128]{3,1,2,0:T(8,128)S(1)}, f32[4,8,1,128]{3,1,2,0:T(8,128)S(1)}, u32[]{:S(2)}, u32[]{:S(2)}) collective-permute-start(f32[4,8,1,128]{3,1,2,0:T(8,128)S(1)} %get-tuple-element.672), channel_id=1, source_target_pairs={{32,0},{64,32},{96,64},{128,96},{160,128},{192,160},{224,192},{0,2... | collective-permute-start | bytes 49160 | tf_op jit(solution)/shard_map/ppermute | solution.py:25
  6.1 7.5 %copy-start.1 = (f32[8,8]{1,0:T(8,128)S(1)}, f32[8,8]{1,0:T(8,128)}, u32[]{:S(2)}) copy-start(f32[8,8]{1,0:T(8,128)} %param.31) | copy-start | bytes 772
  6.2 9.1 %collective-permute-start.6 = (f32[4,8,4,1]{3,1,2,0:T(8,128)S(1)}, f32[4,8,4,1]{3,1,2,0:T(8,128)S(1)}, u32[]{:S(2)}, u32[]{:S(2)}) collective-permute-start(f32[4,8,4,1]{3,1,2,0:T(8,128)S(1)} %get-tuple-element.671), channel_id=1, source_target_pairs={{0,1},{1,2},{2,3},{3,4},{4,5},{5,6},{6,7},{7,8},{8,9},{9,10},{10,1... | collective-permute-start | bytes 1544 | tf_op jit(solution)/shard_map/ppermute | solution.py:24
  7.3 6.5 %copy-start.6 = (s32[4,4,128]{2,1,0:T(4,128)S(1)}, s32[4,4,128]{2,1,0:T(4,128)}, u32[]{:S(2)}) copy-start(s32[4,4,128]{2,1,0:T(4,128)} %param.33) | copy-start | bytes 24580
  7.3 6.6 %copy-start.2 = (f32[64,4,128]{2,1,0:T(4,128)S(1)}, f32[64,4,128]{2,1,0:T(4,128)}, u32[]{:S(2)}) copy-start(f32[64,4,128]{2,1,0:T(4,128)} %param.29) | copy-start | bytes 393220
  7.3 8.1 %collective-permute-start.7 = (f32[4,8,4,1]{3,1,2,0:T(8,128)S(1)}, f32[4,8,4,1]{3,1,2,0:T(8,128)S(1)}, u32[]{:S(2)}, u32[]{:S(2)}) collective-permute-start(f32[4,8,4,1]{3,1,2,0:T(8,128)S(1)} %get-tuple-element.670), channel_id=1, source_target_pairs={{1,0},{2,1},{3,2},{4,3},{5,4},{6,5},{7,6},{8,7},{9,8},{10,9},{11,1... | collective-permute-start | bytes 1544 | tf_op jit(solution)/shard_map/ppermute | solution.py:25
  13.8 0.7 copy-start.4
  15.4 0.9 copy-start.3
  17.7 8.6 %collective-permute-start = (f32[4,8,1,128]{3,1,2,0:T(8,128)S(1)}, f32[4,8,1,128]{3,1,2,0:T(8,128)S(1)}, u32[]{:S(2)}, u32[]{:S(2)}) collective-permute-start(f32[4,8,1,128]{3,1,2,0:T(8,128)S(1)} %get-tuple-element.757), channel_id=1, source_target_pairs={{0,32},{32,64},{64,96},{96,128},{128,160},{160,192},{192,224},{224... | collective-permute-start | bytes 49160 | tf_op jit(solution)/shard_map/while/body/eval_jaxpr/ppermute | solution.py:24
  20.2 6.3 %collective-permute-start.1 = (f32[4,8,1,128]{3,1,2,0:T(8,128)S(1)}, f32[4,8,1,128]{3,1,2,0:T(8,128)S(1)}, u32[]{:S(2)}, u32[]{:S(2)}) collective-permute-start(f32[4,8,1,128]{3,1,2,0:T(8,128)S(1)} %get-tuple-element.759), channel_id=1, source_target_pairs={{32,0},{64,32},{96,64},{128,96},{160,128},{192,160},{224,192},{0,2... | collective-permute-start | bytes 49160 | tf_op jit(solution)/shard_map/while/body/eval_jaxpr/ppermute | solution.py:25
  20.9 6.5 %collective-permute-start.2 = (f32[4,8,4,1]{3,1,2,0:T(8,128)S(1)}, f32[4,8,4,1]{3,1,2,0:T(8,128)S(1)}, u32[]{:S(2)}, u32[]{:S(2)}) collective-permute-start(f32[4,8,4,1]{3,1,2,0:T(8,128)S(1)} %get-tuple-element.763), channel_id=1, source_target_pairs={{0,1},{1,2},{2,3},{3,4},{4,5},{5,6},{6,7},{7,8},{8,9},{9,10},{10,1... | collective-permute-start | bytes 1544 | tf_op jit(solution)/shard_map/while/body/eval_jaxpr/ppermute | solution.py:24
  21.0 6.5 %collective-permute-start.3 = (f32[4,8,4,1]{3,1,2,0:T(8,128)S(1)}, f32[4,8,4,1]{3,1,2,0:T(8,128)S(1)}, u32[]{:S(2)}, u32[]{:S(2)}) collective-permute-start(f32[4,8,4,1]{3,1,2,0:T(8,128)S(1)} %get-tuple-element.765), channel_id=1, source_target_pairs={{1,0},{2,1},{3,2},{4,3},{5,4},{6,5},{7,6},{8,7},{9,8},{10,9},{11,1... | collective-permute-start | bytes 1544 | tf_op jit(solution)/shard_map/while/body/eval_jaxpr/ppermute | solution.py:25
  33.0 15.0 %all-to-all-start = ((f32[32,1,8]{2,1,0:T(1,128)}), f32[32,1,8]{2,1,0:T(1,128)S(1)}, u32[]{:S(2)}, u32[]{:S(2)}) async-start(f32[32,1,8]{2,1,0:T(1,128)} %broadcast_in_dim.147), calls=%async_computation | async-start | bytes 32768 | tf_op jit(solution)/shard_map/while/body/eval_jaxpr/all_to_all | solution.py:32
  48.6 13.5 %all-to-all-start.1 = ((f32[8,1,8]{2,1,0:T(1,128)}), f32[8,1,8]{2,1,0:T(1,128)S(1)}, u32[]{:S(2)}, u32[]{:S(2)}) async-start(f32[8,1,8]{2,1,0:T(1,128)} %broadcast_in_dim.148), calls=%async_computation.1 | async-start | bytes 8192 | tf_op jit(solution)/shard_map/while/body/eval_jaxpr/all_to_all | solution.py:32
  67.1 7.0 %collective-permute-start = (f32[4,8,1,128]{3,1,2,0:T(8,128)S(1)}, f32[4,8,1,128]{3,1,2,0:T(8,128)S(1)}, u32[]{:S(2)}, u32[]{:S(2)}) collective-permute-start(f32[4,8,1,128]{3,1,2,0:T(8,128)S(1)} %get-tuple-element.757), channel_id=1, source_target_pairs={{0,32},{32,64},{64,96},{96,128},{128,160},{160,192},{192,224},{224... | collective-permute-start | bytes 49160 | tf_op jit(solution)/shard_map/while/body/eval_jaxpr/ppermute | solution.py:24
  67.9 6.3 %collective-permute-start.1 = (f32[4,8,1,128]{3,1,2,0:T(8,128)S(1)}, f32[4,8,1,128]{3,1,2,0:T(8,128)S(1)}, u32[]{:S(2)}, u32[]{:S(2)}) collective-permute-start(f32[4,8,1,128]{3,1,2,0:T(8,128)S(1)} %get-tuple-element.759), channel_id=1, source_target_pairs={{32,0},{64,32},{96,64},{128,96},{160,128},{192,160},{224,192},{0,2... | collective-permute-start | bytes 49160 | tf_op jit(solution)/shard_map/while/body/eval_jaxpr/ppermute | solution.py:25
  68.6 6.5 %collective-permute-start.2 = (f32[4,8,4,1]{3,1,2,0:T(8,128)S(1)}, f32[4,8,4,1]{3,1,2,0:T(8,128)S(1)}, u32[]{:S(2)}, u32[]{:S(2)}) collective-permute-start(f32[4,8,4,1]{3,1,2,0:T(8,128)S(1)} %get-tuple-element.763), channel_id=1, source_target_pairs={{0,1},{1,2},{2,3},{3,4},{4,5},{5,6},{6,7},{7,8},{8,9},{9,10},{10,1... | collective-permute-start | bytes 1544 | tf_op jit(solution)/shard_map/while/body/eval_jaxpr/ppermute | solution.py:24
  69.0 6.2 %collective-permute-start.3 = (f32[4,8,4,1]{3,1,2,0:T(8,128)S(1)}, f32[4,8,4,1]{3,1,2,0:T(8,128)S(1)}, u32[]{:S(2)}, u32[]{:S(2)}) collective-permute-start(f32[4,8,4,1]{3,1,2,0:T(8,128)S(1)} %get-tuple-element.765), channel_id=1, source_target_pairs={{1,0},{2,1},{3,2},{4,3},{5,4},{6,5},{7,6},{8,7},{9,8},{10,9},{11,1... | collective-permute-start | bytes 1544 | tf_op jit(solution)/shard_map/while/body/eval_jaxpr/ppermute | solution.py:25
  80.7 15.0 %all-to-all-start = ((f32[32,1,8]{2,1,0:T(1,128)}), f32[32,1,8]{2,1,0:T(1,128)S(1)}, u32[]{:S(2)}, u32[]{:S(2)}) async-start(f32[32,1,8]{2,1,0:T(1,128)} %broadcast_in_dim.147), calls=%async_computation | async-start | bytes 32768 | tf_op jit(solution)/shard_map/while/body/eval_jaxpr/all_to_all | solution.py:32
  96.3 13.4 %all-to-all-start.1 = ((f32[8,1,8]{2,1,0:T(1,128)}), f32[8,1,8]{2,1,0:T(1,128)S(1)}, u32[]{:S(2)}, u32[]{:S(2)}) async-start(f32[8,1,8]{2,1,0:T(1,128)} %broadcast_in_dim.148), calls=%async_computation.1 | async-start | bytes 8192 | tf_op jit(solution)/shard_map/while/body/eval_jaxpr/all_to_all | solution.py:32
  114.6 7.0 %collective-permute-start = (f32[4,8,1,128]{3,1,2,0:T(8,128)S(1)}, f32[4,8,1,128]{3,1,2,0:T(8,128)S(1)}, u32[]{:S(2)}, u32[]{:S(2)}) collective-permute-start(f32[4,8,1,128]{3,1,2,0:T(8,128)S(1)} %get-tuple-element.757), channel_id=1, source_target_pairs={{0,32},{32,64},{64,96},{96,128},{128,160},{160,192},{192,224},{224... | collective-permute-start | bytes 49160 | tf_op jit(solution)/shard_map/while/body/eval_jaxpr/ppermute | solution.py:24
  115.5 6.3 %collective-permute-start.1 = (f32[4,8,1,128]{3,1,2,0:T(8,128)S(1)}, f32[4,8,1,128]{3,1,2,0:T(8,128)S(1)}, u32[]{:S(2)}, u32[]{:S(2)}) collective-permute-start(f32[4,8,1,128]{3,1,2,0:T(8,128)S(1)} %get-tuple-element.759), channel_id=1, source_target_pairs={{32,0},{64,32},{96,64},{128,96},{160,128},{192,160},{224,192},{0,2... | collective-permute-start | bytes 49160 | tf_op jit(solution)/shard_map/while/body/eval_jaxpr/ppermute | solution.py:25
  116.2 6.5 %collective-permute-start.2 = (f32[4,8,4,1]{3,1,2,0:T(8,128)S(1)}, f32[4,8,4,1]{3,1,2,0:T(8,128)S(1)}, u32[]{:S(2)}, u32[]{:S(2)}) collective-permute-start(f32[4,8,4,1]{3,1,2,0:T(8,128)S(1)} %get-tuple-element.763), channel_id=1, source_target_pairs={{0,1},{1,2},{2,3},{3,4},{4,5},{5,6},{6,7},{7,8},{8,9},{9,10},{10,1... | collective-permute-start | bytes 1544 | tf_op jit(solution)/shard_map/while/body/eval_jaxpr/ppermute | solution.py:24
  116.6 6.2 %collective-permute-start.3 = (f32[4,8,4,1]{3,1,2,0:T(8,128)S(1)}, f32[4,8,4,1]{3,1,2,0:T(8,128)S(1)}, u32[]{:S(2)}, u32[]{:S(2)}) collective-permute-start(f32[4,8,4,1]{3,1,2,0:T(8,128)S(1)} %get-tuple-element.765), channel_id=1, source_target_pairs={{1,0},{2,1},{3,2},{4,3},{5,4},{6,5},{7,6},{8,7},{9,8},{10,9},{11,1... | collective-permute-start | bytes 1544 | tf_op jit(solution)/shard_map/while/body/eval_jaxpr/ppermute | solution.py:25
  128.3 15.0 %all-to-all-start = ((f32[32,1,8]{2,1,0:T(1,128)}), f32[32,1,8]{2,1,0:T(1,128)S(1)}, u32[]{:S(2)}, u32[]{:S(2)}) async-start(f32[32,1,8]{2,1,0:T(1,128)} %broadcast_in_dim.147), calls=%async_computation | async-start | bytes 32768 | tf_op jit(solution)/shard_map/while/body/eval_jaxpr/all_to_all | solution.py:32
  143.9 13.4 %all-to-all-start.1 = ((f32[8,1,8]{2,1,0:T(1,128)}), f32[8,1,8]{2,1,0:T(1,128)S(1)}, u32[]{:S(2)}, u32[]{:S(2)}) async-start(f32[8,1,8]{2,1,0:T(1,128)} %broadcast_in_dim.148), calls=%async_computation.1 | async-start | bytes 8192 | tf_op jit(solution)/shard_map/while/body/eval_jaxpr/all_to_all | solution.py:32
  162.2 7.0 %collective-permute-start = (f32[4,8,1,128]{3,1,2,0:T(8,128)S(1)}, f32[4,8,1,128]{3,1,2,0:T(8,128)S(1)}, u32[]{:S(2)}, u32[]{:S(2)}) collective-permute-start(f32[4,8,1,128]{3,1,2,0:T(8,128)S(1)} %get-tuple-element.757), channel_id=1, source_target_pairs={{0,32},{32,64},{64,96},{96,128},{128,160},{160,192},{192,224},{224... | collective-permute-start | bytes 49160 | tf_op jit(solution)/shard_map/while/body/eval_jaxpr/ppermute | solution.py:24
  163.1 6.3 %collective-permute-start.1 = (f32[4,8,1,128]{3,1,2,0:T(8,128)S(1)}, f32[4,8,1,128]{3,1,2,0:T(8,128)S(1)}, u32[]{:S(2)}, u32[]{:S(2)}) collective-permute-start(f32[4,8,1,128]{3,1,2,0:T(8,128)S(1)} %get-tuple-element.759), channel_id=1, source_target_pairs={{32,0},{64,32},{96,64},{128,96},{160,128},{192,160},{224,192},{0,2... | collective-permute-start | bytes 49160 | tf_op jit(solution)/shard_map/while/body/eval_jaxpr/ppermute | solution.py:25
  163.8 6.5 %collective-permute-start.2 = (f32[4,8,4,1]{3,1,2,0:T(8,128)S(1)}, f32[4,8,4,1]{3,1,2,0:T(8,128)S(1)}, u32[]{:S(2)}, u32[]{:S(2)}) collective-permute-start(f32[4,8,4,1]{3,1,2,0:T(8,128)S(1)} %get-tuple-element.763), channel_id=1, source_target_pairs={{0,1},{1,2},{2,3},{3,4},{4,5},{5,6},{6,7},{7,8},{8,9},{9,10},{10,1... | collective-permute-start | bytes 1544 | tf_op jit(solution)/shard_map/while/body/eval_jaxpr/ppermute | solution.py:24
  164.2 6.2 %collective-permute-start.3 = (f32[4,8,4,1]{3,1,2,0:T(8,128)S(1)}, f32[4,8,4,1]{3,1,2,0:T(8,128)S(1)}, u32[]{:S(2)}, u32[]{:S(2)}) collective-permute-start(f32[4,8,4,1]{3,1,2,0:T(8,128)S(1)} %get-tuple-element.765), channel_id=1, source_target_pairs={{1,0},{2,1},{3,2},{4,3},{5,4},{6,5},{7,6},{8,7},{9,8},{10,9},{11,1... | collective-permute-start | bytes 1544 | tf_op jit(solution)/shard_map/while/body/eval_jaxpr/ppermute | solution.py:25
  175.9 15.0 %all-to-all-start = ((f32[32,1,8]{2,1,0:T(1,128)}), f32[32,1,8]{2,1,0:T(1,128)S(1)}, u32[]{:S(2)}, u32[]{:S(2)}) async-start(f32[32,1,8]{2,1,0:T(1,128)} %broadcast_in_dim.147), calls=%async_computation | async-start | bytes 32768 | tf_op jit(solution)/shard_map/while/body/eval_jaxpr/all_to_all | solution.py:32
  191.5 13.4 %all-to-all-start.1 = ((f32[8,1,8]{2,1,0:T(1,128)}), f32[8,1,8]{2,1,0:T(1,128)S(1)}, u32[]{:S(2)}, u32[]{:S(2)}) async-start(f32[8,1,8]{2,1,0:T(1,128)} %broadcast_in_dim.148), calls=%async_computation.1 | async-start | bytes 8192 | tf_op jit(solution)/shard_map/while/body/eval_jaxpr/all_to_all | solution.py:32
  209.8 7.0 %collective-permute-start = (f32[4,8,1,128]{3,1,2,0:T(8,128)S(1)}, f32[4,8,1,128]{3,1,2,0:T(8,128)S(1)}, u32[]{:S(2)}, u32[]{:S(2)}) collective-permute-start(f32[4,8,1,128]{3,1,2,0:T(8,128)S(1)} %get-tuple-element.757), channel_id=1, source_target_pairs={{0,32},{32,64},{64,96},{96,128},{128,160},{160,192},{192,224},{224... | collective-permute-start | bytes 49160 | tf_op jit(solution)/shard_map/while/body/eval_jaxpr/ppermute | solution.py:24
  210.7 6.3 %collective-permute-start.1 = (f32[4,8,1,128]{3,1,2,0:T(8,128)S(1)}, f32[4,8,1,128]{3,1,2,0:T(8,128)S(1)}, u32[]{:S(2)}, u32[]{:S(2)}) collective-permute-start(f32[4,8,1,128]{3,1,2,0:T(8,128)S(1)} %get-tuple-element.759), channel_id=1, source_target_pairs={{32,0},{64,32},{96,64},{128,96},{160,128},{192,160},{224,192},{0,2... | collective-permute-start | bytes 49160 | tf_op jit(solution)/shard_map/while/body/eval_jaxpr/ppermute | solution.py:25
  211.3 6.5 %collective-permute-start.2 = (f32[4,8,4,1]{3,1,2,0:T(8,128)S(1)}, f32[4,8,4,1]{3,1,2,0:T(8,128)S(1)}, u32[]{:S(2)}, u32[]{:S(2)}) collective-permute-start(f32[4,8,4,1]{3,1,2,0:T(8,128)S(1)} %get-tuple-element.763), channel_id=1, source_target_pairs={{0,1},{1,2},{2,3},{3,4},{4,5},{5,6},{6,7},{7,8},{8,9},{9,10},{10,1... | collective-permute-start | bytes 1544 | tf_op jit(solution)/shard_map/while/body/eval_jaxpr/ppermute | solution.py:24
  211.7 6.2 %collective-permute-start.3 = (f32[4,8,4,1]{3,1,2,0:T(8,128)S(1)}, f32[4,8,4,1]{3,1,2,0:T(8,128)S(1)}, u32[]{:S(2)}, u32[]{:S(2)}) collective-permute-start(f32[4,8,4,1]{3,1,2,0:T(8,128)S(1)} %get-tuple-element.765), channel_id=1, source_target_pairs={{1,0},{2,1},{3,2},{4,3},{5,4},{6,5},{7,6},{8,7},{9,8},{10,9},{11,1... | collective-permute-start | bytes 1544 | tf_op jit(solution)/shard_map/while/body/eval_jaxpr/ppermute | solution.py:25
  223.4 15.0 %all-to-all-start = ((f32[32,1,8]{2,1,0:T(1,128)}), f32[32,1,8]{2,1,0:T(1,128)S(1)}, u32[]{:S(2)}, u32[]{:S(2)}) async-start(f32[32,1,8]{2,1,0:T(1,128)} %broadcast_in_dim.147), calls=%async_computation | async-start | bytes 32768 | tf_op jit(solution)/shard_map/while/body/eval_jaxpr/all_to_all | solution.py:32
  239.0 13.4 %all-to-all-start.1 = ((f32[8,1,8]{2,1,0:T(1,128)}), f32[8,1,8]{2,1,0:T(1,128)S(1)}, u32[]{:S(2)}, u32[]{:S(2)}) async-start(f32[8,1,8]{2,1,0:T(1,128)} %broadcast_in_dim.148), calls=%async_computation.1 | async-start | bytes 8192 | tf_op jit(solution)/shard_map/while/body/eval_jaxpr/all_to_all | solution.py:32
  258.6 12.4 %all-to-all-start.2 = ((f32[32,1,1]{2,1,0:T(1,128)}), f32[32,1,1]{2,1,0:T(1,128)S(1)}, u32[]{:S(2)}, u32[]{:S(2)}) async-start(f32[32,1,1]{2,1,0:T(1,128)} %broadcast_in_dim.113), calls=%async_computation.2 | async-start | bytes 32768 | tf_op jit(solution)/shard_map/all_to_all | solution.py:32
  282.5 0.9 copy-start
where the time goes:
time: 284 us; the launch traced here: 283 us
  starting transfers between devices  121 us (43%)
  waiting for transfers between devices  77.4 us (27%)
  matrix products  30.1 us (11%)
  other arithmetic  19.2 us (7%)
  local copies, waits for them, and re-layouts  17.2 us (6%)
  blocking collectives  8.79 us (3%)
  loops' own time  8.09 us (3%)
    all_to_all x11, starting transfers between devices, sent_to_all(): return lax.all_to_all(copies, axis, split_axis=0, concat_axis=0, tiled=True)  80 us
    all_to_all x11, waiting for transfers between devices, sent_to_all(): return lax.all_to_all(copies, axis, split_axis=0, concat_axis=0, tiled=True)  73.7 us
    ppermute x12, starting transfers between devices, extended(): after = lax.ppermute(leading, axis, down)  29.4 us
    dot_general x5, matrix products, products(): per_cell = jnp.einsum('kqxy,qxy->kxy', basis, image, precision=highest)  13.2 us
    ppermute x12, starting transfers between devices, extended(): before = lax.ppermute(last, axis, up)  11.4 us
    all_to_all x1, blocking collectives, sent_to_all(): return lax.all_to_all(copies, axis, split_axis=0, concat_axis=0, tiled=True)  8.79 us
    reduce_sum x12, other arithmetic, local_total(): return jnp.sum(jnp.sum(values, axis=0))  8.12 us
    another operation x1, loops' own time, body(): lax.fori_loop(0, ITERS, advance, (basis, hessen, first))  8.09 us
  transfers between devices with their start and end apart: 35, of which 16 were waited for; matrix products, arithmetic and copies ran while one was open for 3% of the time, Pallas kernels for 0%

commit v1 on v0

--- a/solution.py
+++ b/solution.py
@@ -1,6 +1,10 @@
+import functools
+
 import jax
 import jax.numpy as jnp
 from jax import lax
+from jax.experimental import pallas as pl
+from jax.experimental.pallas import tpu as pltpu
 from jax.sharding import Mesh
 from jax.sharding import PartitionSpec as P
 
@@ -104,7 +108,7 @@
     return jnp.sqrt(squares / total + FLOOR)
 
 
-def body(source, initial, reaction, stiffness, line_op, face_deriv, wall_flags):
+def stepwise(source, initial, reaction, stiffness, line_op, face_deriv, wall_flags):
     highest = lax.Precision.HIGHEST
     total = float(
         P_SIZE * P_SIZE * source.shape[1] * lax.axis_size(GX) * source.shape[2] * lax.axis_size(GY)
@@ -148,6 +152,370 @@
     basis = basis.at[ITERS].set(pending / beta)
     hessen = hessen + jnp.where((rows == ITERS) & (cols == ITERS - 1), beta, 0.0)
     return (hessen, basis)
+
+
+NODES = P_SIZE * P_SIZE
+ROWS = 16
+DEPTH = 6
+LANES = 128
+SCALE = 0.125
+AMP_LIMIT = 100.0
+GRAM = [(k, l) for k in range(ITERS + 1) for l in range(k + 1)]
+HIGHEST = lax.Precision.HIGHEST
+
+
+def centre(line_ref, deriv_ref):
+    trace = line_ref[0, 0]
+    for a in range(1, P_SIZE):
+        trace = trace + line_ref[a, a]
+    return 2.0 + 0.3125 * trace + 0.5 * (TAU + 0.5 * deriv_ref[0])
+
+
+def lane_ids(rows):
+    return lax.broadcasted_iota(jnp.int32, (rows, LANES), 1)
+
+
+def turned(value, shift):
+    shift = shift % LANES
+    return value if shift == 0 else pltpu.roll(value, shift, 1)
+
+
+def strided(ref, start, count):
+    return ref[pl.ds(start, count, stride=4), :]
+
+
+def pack_kernel(source, initial, reaction, stiffness, walls, near, low2, high2, to_up, to_down):
+    opened = 1.0 - walls[...].astype(jnp.float32)
+    near[0:256, :] = initial[...]
+    near[256:512, :] = source[...]
+    near[512:768, :] = reaction[...]
+    near[768:772, :] = stiffness[...]
+    near[772:788, :] = opened
+    near[788:792, :] = jnp.zeros((4, LANES), jnp.float32)
+    for out, far, close in ((high2, 2, 3), (low2, 1, 0)):
+        out[0:64, :] = strided(initial, far, NODES)
+        out[64:128, :] = strided(initial, close, NODES)
+        out[128:192, :] = strided(source, close, NODES)
+        out[192:256, :] = strided(reaction, close, NODES)
+        out[256:257, :] = stiffness[close : close + 1, :]
+        for f in range(4):
+            out[257 + f : 258 + f, :] = opened[4 * f + close : 4 * f + close + 1, :]
+        out[261:264, :] = jnp.zeros((3, LANES), jnp.float32)
+    lanes = lane_ids(NODES)
+    lanes8 = lane_ids(8)
+    for out, first in ((to_up, 120), (to_down, 0)):
+        total = jnp.zeros((NODES, LANES), jnp.float32)
+        extra = jnp.zeros((8, LANES), jnp.float32)
+        for x in range(4):
+            for field, ref in enumerate((initial, source, reaction)):
+                at = 32 * field + 8 * x
+                moved = turned(strided(ref, x, NODES), at - first)
+                total = jnp.where((lanes >= at) & (lanes < at + 8), moved, total)
+            at = 96 + 8 * x
+            rows = [stiffness[x : x + 1, :]] + [opened[4 * f + x : 4 * f + x + 1, :] for f in range(4)]
+            rows = jnp.concatenate(rows + [jnp.zeros((3, LANES), jnp.float32)], axis=0)
+            extra = jnp.where((lanes8 >= at) & (lanes8 < at + 8), turned(rows, at - first), extra)
+        out[...] = total
+        out[0:8, :] = total[0:8] + extra
+
+
+def weights_in(line_ref, deriv_ref):
+    def grid(rows, columns):
+        return (
+            lax.broadcasted_iota(jnp.int32, (rows, columns), 0),
+            lax.broadcasted_iota(jnp.int32, (rows, columns), 1),
+        )
+
+    r, s = grid(NODES, NODES)
+    ra, rb, sa, sb = r // 8, r % 8, s // 8, s % 8
+    full = jnp.zeros((NODES, NODES), jnp.float32)
+    for a in range(P_SIZE):
+        for c in range(P_SIZE):
+            value = line_ref[a, c]
+            full = full + jnp.where((ra == a) & (sa == c) & (rb == sb), value, 0.0)
+            full = full + jnp.where((rb == a) & (sb == c) & (ra == sa), value, 0.0)
+    r, s = grid(8, NODES)
+    sa, sb = s // 8, s % 8
+    parts = [full]
+    for along, across in ((sa, sb), (sb, sa)):
+        for flip in (False, True):
+            part = jnp.zeros((8, NODES), jnp.float32)
+            for c in range(P_SIZE):
+                value = 0.5 * deriv_ref[c] + (TAU if c == 0 else 0.0)
+                place = P_SIZE - 1 - c if flip else c
+                part = part + jnp.where((across == r) & (along == place), value, 0.0)
+            parts.append(part * SCALE)
+    return jnp.concatenate(parts, axis=0)
+
+
+def powers_kernel(
+    line_ref, deriv_ref, source, initial, reaction, stiffness, walls,
+    below1, above1, below2, above2, own_strip, strip_b1, strip_a1, strip_b2, strip_a2,
+    basis_out, gram_out, field_a, field_b, weight, image, react, stiff, opened,
+):
+    shift = centre(line_ref, deriv_ref)
+    weight[...] = weights_in(line_ref, deriv_ref)
+
+    def put(row, value_initial, value_reaction, value_stiffness, value_open):
+        cols = slice(row * LANES, (row + 1) * LANES)
+        field_a[:, cols] = value_initial
+        react[:, cols] = (value_reaction - shift) * SCALE
+        stiff[:, cols] = jnp.broadcast_to(value_stiffness * SCALE, (8, LANES))
+        for f in range(4):
+            opened[8 * f : 8 * f + 8, cols] = jnp.broadcast_to(value_open[f], (8, LANES))
+
+    own_open = 1.0 - walls[...].astype(jnp.float32)
+    for x in range(4):
+        put(
+            6 + x, strided(initial, x, NODES), strided(reaction, x, NODES), stiffness[x : x + 1, :],
+            [own_open[4 * f + x : 4 * f + x + 1, :] for f in range(4)],
+        )
+        for ref, row in ((below1, 2 + x), (above1, 10 + x)):
+            put(
+                row, strided(ref, x, NODES), strided(ref, 512 + x, NODES), ref[768 + x : 769 + x, :],
+                [ref[772 + 4 * f + x : 773 + 4 * f + x, :] for f in range(4)],
+            )
+    for ref, far, close in ((below2, 0, 1), (above2, 15, 14)):
+        put(
+            close, ref[64:128, :], ref[192:256, :], ref[256:257, :],
+            [ref[257 + f : 258 + f, :] for f in range(4)],
+        )
+        field_a[:, far * LANES : (far + 1) * LANES] = ref[0:64, :]
+
+    lanes64 = lane_ids(NODES)
+    lanes = lane_ids(8)
+    pieces = ((strip_b2, 0, 16, -16), (strip_b1, 16, 48, 16), (own_strip, 48, 80, 48),
+              (strip_a1, 80, 112, 80), (strip_a2, 112, 128, 112))
+    strip_source = []
+    for side in range(2):
+        rows = slice(NODES * side, NODES * side + NODES)
+        made = []
+        for field in range(4):
+            count = NODES if field < 3 else 8
+            ids = lanes64 if field < 3 else lanes
+            value = jnp.zeros((count, LANES), jnp.float32)
+            for ref, start, stop, zero in pieces:
+                part = ref[NODES * side : NODES * side + count, :]
+                value = jnp.where((ids >= start) & (ids < stop), turned(part, zero - 32 * field), value)
+            made.append(value)
+        put(ROWS + side, made[0], made[2], made[3][0:1], [made[3][1 + f : 2 + f] for f in range(4)])
+        strip_source.append(made[1])
+
+    def columns(row):
+        return slice(row * LANES, (row + 1) * LANES)
+
+    low, high = ROWS, ROWS + 1
+    sub = lax.broadcasted_iota(jnp.int32, (8, LANES), 0)
+    TW, TE, TS, TN = (slice(64 + 8 * f, 72 + 8 * f) for f in range(4))
+
+    def source_of(row):
+        if row >= ROWS:
+            return strip_source[row - ROWS]
+        if 6 <= row < 10:
+            return strided(source, row - 6, NODES)
+        if 2 <= row < 6:
+            return strided(below1, 256 + row - 2, NODES)
+        if 10 <= row < 14:
+            return strided(above1, 256 + row - 10, NODES)
+        return (below2 if row < 2 else above2)[128:192, :]
+
+    def apply(old, new, step, first):
+        start, stop = step, ROWS - step
+        image[:, start * LANES : stop * LANES] = jnp.dot(
+            weight[...], old[:, start * LANES : stop * LANES],
+            precision=HIGHEST, preferred_element_type=jnp.float32,
+        )
+        image[:, ROWS * LANES : (ROWS + 2) * LANES] = jnp.dot(
+            weight[...], old[:, ROWS * LANES : (ROWS + 2) * LANES],
+            precision=HIGHEST, preferred_element_type=jnp.float32,
+        )
+
+        def finish(row, from_west, from_east, from_south, from_north):
+            cols = columns(row)
+            west = image[TW, cols] - opened[0:8, cols] * from_west
+            east = image[TE, cols] - opened[8:16, cols] * from_east
+            south = image[TS, cols] - opened[16:24, cols] * from_south
+            north = image[TN, cols] - opened[24:32, cols] * from_north
+            for a in range(P_SIZE):
+                rows = slice(8 * a, 8 * a + 8)
+                value = react[rows, cols] * old[rows, cols] + stiff[:, cols] * image[rows, cols]
+                if a == 0:
+                    value = value + west
+                if a == P_SIZE - 1:
+                    value = value + east
+                edge = jnp.where(sub == 0, south[a : a + 1, :], 0.0)
+                edge = jnp.where(sub == P_SIZE - 1, north[a : a + 1, :], edge)
+                value = value + edge
+                if first:
+                    value = -8.0 * value - shift * old[rows, cols]
+                new[rows, cols] = value
+            if first:
+                new[:, cols] = new[:, cols] + source_of(row)
+
+        north_low = image[TN, columns(low)]
+        south_high = image[TS, columns(high)]
+        for row in range(start + 1, stop - 1):
+            cols = columns(row)
+            from_south = jnp.where(
+                lanes == 0, turned(north_low, -(8 * row + 7)), turned(image[TN, cols], 1)
+            )
+            from_north = jnp.where(
+                lanes == LANES - 1, turned(south_high, 127 - 8 * row), turned(image[TS, cols], -1)
+            )
+            finish(row, image[TE, columns(row - 1)], image[TW, columns(row + 1)], from_south, from_north)
+        if step == DEPTH - 1:
+            return
+        to_low = turned(image[TS, columns(low)], -1)
+        to_high = turned(image[TN, columns(high)], 1)
+        for row in range(start, stop):
+            cols = columns(row)
+            to_low = jnp.where(lanes == 8 * row + 7, turned(image[TS, cols], 8 * row + 7), to_low)
+            to_high = jnp.where(lanes == 8 * row, turned(image[TN, cols], 8 * row + 1), to_high)
+        cols = columns(low)
+        finish(low, turned(image[TE, cols], 8), turned(image[TW, cols], -8), turned(image[TN, cols], 1), to_low)
+        cols = columns(high)
+        finish(high, turned(image[TE, cols], 8), turned(image[TW, cols], -8), to_high, turned(image[TS, cols], -1))
+
+    old, new = field_a, field_b
+    for step in range(DEPTH):
+        apply(old, new, step, step == 0)
+        basis_out[step, :, :] = new[:, 6 * LANES : 10 * LANES]
+        old, new = new, old
+
+    sums = [jnp.zeros((8, LANES), jnp.float32) for _ in GRAM]
+    for x in range(4):
+        for a in range(P_SIZE):
+            values = [basis_out[k, 8 * a : 8 * a + 8, x * LANES : (x + 1) * LANES] for k in range(ITERS + 1)]
+            sums = [total + values[k] * values[l] for total, (k, l) in zip(sums, GRAM)]
+    rows = [jnp.sum(total, axis=0, keepdims=True) for total in sums]
+    rows = jnp.concatenate(rows + [jnp.zeros((24 - len(GRAM), LANES), jnp.float32)], axis=0)
+    totals = jnp.sum(rows, axis=1, keepdims=True)
+    place = lax.broadcasted_iota(jnp.int32, (24, LANES), 0) == lax.broadcasted_iota(jnp.int32, (24, LANES), 1)
+    gram_out[...] = jnp.sum(jnp.where(place, totals, 0.0), axis=0, keepdims=True)
+
+
+def combine_kernel(nodes, line_ref, deriv_ref, powers, gathered, basis_out, hess_out, amp_out):
+    shift = centre(line_ref, deriv_ref)
+    row = jnp.sum(gathered[...], axis=0, keepdims=True) * (1.0 / nodes)
+    spread = jnp.broadcast_to(row, (8, LANES))
+    gram = {}
+    for at, (k, l) in enumerate(GRAM):
+        gram[k, l] = gram[l, k] = jnp.broadcast_to(spread[:, at : at + 1], (8, LANES))
+    sizes = [jnp.sqrt(gram[k, k]) for k in range(ITERS + 1)]
+    sub = lax.broadcasted_iota(jnp.int32, (8, LANES), 0)
+    lanes = lane_ids(8)
+    hess = jnp.zeros((8, LANES), jnp.float32)
+    beta = jnp.sqrt(gram[0, 0] + FLOOR)
+    coeffs = [[1.0 / beta]]
+    amp = sizes[0] * coeffs[0][0]
+
+    def put(hess, i, j, value):
+        return jnp.where((sub == i) & (lanes == j), value, hess)
+
+    for j in range(ITERS):
+        last = coeffs[j]
+        image = [shift * c for c in last] + [None]
+        for k in range(j + 1):
+            moved = last[k] * 8.0
+            image[k + 1] = moved if image[k + 1] is None else image[k + 1] + moved
+        weighted = [
+            sum(gram[k, l] * image[l] for l in range(1, j + 2)) + gram[k, 0] * image[0] for k in range(j + 2)
+        ]
+        pending = list(image)
+        for i in range(j + 1):
+            h = sum(c * weighted[k] for k, c in enumerate(coeffs[i]))
+            hess = put(hess, i, j, h)
+            for k, c in enumerate(coeffs[i]):
+                pending[k] = pending[k] - h * c
+        square = sum(
+            pending[k] * sum(gram[k, l] * pending[l] for l in range(j + 2)) for k in range(j + 2)
+        )
+        beta = jnp.sqrt(jnp.maximum(square, 0.0) + FLOOR)
+        hess = put(hess, j + 1, j, beta)
+        scale = 1.0 / beta
+        coeffs.append([p * scale for p in pending])
+        amp = jnp.maximum(amp, sum(jnp.abs(c) * s for c, s in zip(coeffs[-1], sizes)))
+    hess_out[...] = hess[0 : ITERS + 1, 0:ITERS]
+    amp_out[...] = amp[0:1, :]
+    for x in range(4):
+        for a in range(P_SIZE):
+            values = [powers[k, 8 * a : 8 * a + 8, x * LANES : (x + 1) * LANES] for k in range(ITERS + 1)]
+            for j in range(ITERS + 1):
+                total = coeffs[j][0] * values[0]
+                for k in range(1, j + 1):
+                    total = total + coeffs[j][k] * values[k]
+                basis_out[j, pl.ds(32 * a + x, 8, stride=4), :] = total
+
+
+def fast(source, initial, reaction, stiffness, line_op, face_deriv, wall_flags):
+    vmem = pl.BlockSpec(memory_space=pltpu.VMEM)
+    smem = pl.BlockSpec(memory_space=pltpu.SMEM)
+    f32 = jnp.float32
+    flat = [v.reshape(4 * NODES, LANES) for v in (source, initial, reaction)]
+    walls = wall_flags.reshape(16, LANES)
+    nx, ny = lax.axis_size(GX), lax.axis_size(GY)
+
+    def moved(value, axis, size, by):
+        return lax.ppermute(value, axis, [(i, (i + by) % size) for i in range(size)])
+
+    near, low2, high2, to_up, to_down = pl.pallas_call(
+        pack_kernel,
+        out_shape=[jax.ShapeDtypeStruct((n, LANES), f32) for n in (792, 264, 264, NODES, NODES)],
+        in_specs=[vmem] * 5,
+        out_specs=[vmem] * 5,
+    )(*flat, stiffness, walls)
+    below1 = moved(near, GX, nx, 1)
+    above1 = moved(near, GX, nx, -1)
+    below2 = moved(high2, GX, nx, 2)
+    above2 = moved(low2, GX, nx, -2)
+    left = moved(to_up, GY, ny, 1)
+    right = moved(to_down, GY, ny, -1)
+    own_strip = jnp.concatenate([left, right], axis=0)
+    strips = [moved(own_strip, GX, nx, by) for by in (1, -1, 2, -2)]
+
+    powers, gram = pl.pallas_call(
+        powers_kernel,
+        out_shape=[
+            jax.ShapeDtypeStruct((ITERS + 1, NODES, 4 * LANES), f32),
+            jax.ShapeDtypeStruct((1, LANES), f32),
+        ],
+        in_specs=[smem, smem] + [vmem] * 14,
+        out_specs=[vmem] * 2,
+        scratch_shapes=[
+            pltpu.VMEM((NODES, (ROWS + 2) * LANES), f32),
+            pltpu.VMEM((NODES, (ROWS + 2) * LANES), f32),
+            pltpu.VMEM((NODES + 32, NODES), f32),
+            pltpu.VMEM((NODES + 32, (ROWS + 2) * LANES), f32),
+            pltpu.VMEM((NODES, (ROWS + 2) * LANES), f32),
+            pltpu.VMEM((8, (ROWS + 2) * LANES), f32),
+            pltpu.VMEM((32, (ROWS + 2) * LANES), f32),
+        ],
+    )(line_op, face_deriv, *flat, stiffness, walls, below1, above1, below2, above2, own_strip, *strips)
+    every = GX + GY
+    copies = jnp.broadcast_to(gram, (nx * ny, LANES))
+    gathered = lax.all_to_all(copies, every, split_axis=0, concat_axis=0, tiled=True)
+    basis, hess, amp = pl.pallas_call(
+        functools.partial(combine_kernel, float(NODES * 4 * nx * LANES * ny)),
+        out_shape=[
+            jax.ShapeDtypeStruct((ITERS + 1, 4 * NODES, LANES), f32),
+            jax.ShapeDtypeStruct((ITERS + 1, ITERS), f32),
+            jax.ShapeDtypeStruct((1, LANES), f32),
+        ],
+        in_specs=[smem, smem] + [vmem] * 2,
+        out_specs=[vmem] * 3,
+    )(line_op, face_deriv, powers, gathered)
+    return hess, basis.reshape(ITERS + 1, NODES, 4, LANES), amp[0, 0]
+
+
+def body(*args):
+    hess, basis, amp = fast(*args)
+
+    def again(carry):
+        return (jnp.bool_(True),) + stepwise(*args)
+
+    done = amp <= AMP_LIMIT
+    _, hess, basis = lax.while_loop(lambda carry: jnp.logical_not(carry[0]), again, (done, hess, basis))
+    return (hess, basis)
 
 
 def solution(mesh):

time: 284 us -> 74.2 us (0.26)
  starting transfers between devices: 121 us -> 31 us
  waiting for transfers between devices: 77.4 us -> 18.7 us
  matrix products: 30.1 us -> 0 us
  other arithmetic: 19.2 us -> 0 us
  Pallas kernels: 0 us -> 11.8 us
  blocking collectives: 8.79 us -> 0 us
  loops' own time: 8.09 us -> 0.19 us
  local copies, waits for them, and re-layouts: 17.2 us -> 11.4 us
    all_to_all x11 -> x1, starting transfers between devices: 80 us -> 11.5 us  [fast(): lax.all_to_all(copies, every, split_axis=0, concat_axis=0, tiled=True)]
    all_to_all x11 -> x1, waiting for transfers between devices: 73.7 us -> 11.2 us  [fast(): lax.all_to_all(copies, every, split_axis=0, concat_axis=0, tiled=True)]
    dot_general x46 -> x0, matrix products: 30.1 us -> none  [the longest x5 13.2 us: products(): per_cell = jnp.einsum('kqxy,qxy->kxy', basis, image, precision=highest)]
    ppermute x24 -> x10, starting transfers between devices: 40.9 us -> 19.4 us  [moved(): lax.ppermute(value, axis, [(i, (i + by) % size) for i in range(size)])]
    pallas_call x0 -> x3, Pallas kernels: none -> 11.8 us  [the longest x1 7.21 us: fast(): pl.pallas_call(powers_kernel, out_shape=[jax.ShapeDtypeStruct((ITERS + 1,...]
    reduce_sum x24 -> x0, other arithmetic: 9.72 us -> none  [the longest x12 8.12 us: local_total(): return jnp.sum(jnp.sum(values, axis=0))]
    all_to_all x1 -> x0, blocking collectives: 8.79 us -> none  [sent_to_all(): return lax.all_to_all(copies, axis, split_axis=0, concat_axis=0, tiled=True)]
    another operation x1, loops' own time: 8.09 us -> 0.19 us  [body(): lax.while_loop(lambda carry: jnp.logical_not(carry[0]), again, (done, hes...]
  transfers between devices with their start and end apart: 35 -> 11, of which waited for: 16 -> 5; matrix products, arithmetic and copies ran while one was open for 3% -> 0% of each run, Pallas kernels for 0% -> 0%
where the time goes in v1:
time: 74.2 us; the launch traced here: 73.9 us
  starting transfers between devices  31 us (42%)
  waiting for transfers between devices  18.7 us (25%)
  Pallas kernels  11.8 us (16%)
  local copies, waits for them, and re-layouts  11.4 us (15%)
  between operations  0.83 us (1%)
    ppermute x10, starting transfers between devices, moved(): lax.ppermute(value, axis, [(i, (i + by) % size) for i in range(size)])  19.4 us
    all_to_all x1, starting transfers between devices, fast(): lax.all_to_all(copies, every, split_axis=0, concat_axis=0, tiled=True)  11.5 us
    all_to_all x1, waiting for transfers between devices, fast(): lax.all_to_all(copies, every, split_axis=0, concat_axis=0, tiled=True)  11.2 us
    unnamed x40, local copies, waits for them, and re-layouts  8.51 us
    ppermute x10, waiting for transfers between devices, moved(): lax.ppermute(value, axis, [(i, (i + by) % size) for i in range(size)])  7.52 us
    pallas_call x1, Pallas kernels, fast(): pl.pallas_call(powers_kernel, out_shape=[jax.ShapeDtypeStruct((ITERS + 1,...  7.21 us
    pallas_call x1, Pallas kernels, fast(): pl.pallas_call(functools.partial(combine_kernel, float(NODES * 4 * nx * L...  2.47 us
    while x4, local copies, waits for them, and re-layouts, body(): lax.while_loop(lambda carry: jnp.logical_not(carry[0]), again, (done, hes...  2.16 us
  transfers between devices with their start and end apart: 11, of which 5 were waited for; matrix products, arithmetic and copies ran while one was open for 0% of the time, Pallas kernels for 0%

profile of v1, /device:TPU:1, one launch (start us, length us, event | category | flops | bytes accessed | tf_op | source)
XLA Modules:
  0.0 73.9 jit_solution(2256187117202485439)
XLA Ops:
  0.6 0.0 copy-start.2
  0.6 0.7 copy-done.2
  1.3 2.1 %shard_map.86 = (f32[792,128]{1,0:T(8,128)}, f32[264,128]{1,0:T(8,128)}, f32[264,128]{1,0:T(8,128)}, f32[64,128]{1,0:T(8,128)}, f32[64,128]{1,0:T(8,128)}) custom-call(f32[256,128]{1,0:T(8,128)} %bitcast.519, f32[256,128]{1,0:T(8,128)} %bitcast.517, f32[256,128]{1,0:T(8,128)} %bitcast.515, f32[4,128]{1,0:T(4,128)S(1)} %copy-done.2, s32[16,128]{1,0:T(8,128)} %bitcast.523), custom_call_target="tpu_custom_call" | custom-call | tf_op jit(solution)/shard_map/pallas_call | solution.py:461
  3.4 2.5 %collective-permute-start.12 = (f32[64,128]{1,0:T(8,128)}, f32[64,128]{1,0:T(8,128)S(1)}, u32[]{:S(2)}, u32[]{:S(2)}) collective-permute-start(f32[64,128]{1,0:T(8,128)} %get-tuple-element.549), channel_id=1, source_target_pairs={{0,1},{1,2},{2,3},{3,4},{4,5},{5,6},{6,7},{7,8},{8,9},{9,10},{10,1... | collective-permute-start | bytes 98312 | tf_op jit(solution)/shard_map/ppermute | solution.py:459
  5.8 2.1 %collective-permute-start.8 = (f32[792,128]{1,0:T(8,128)}, f32[792,128]{1,0:T(8,128)S(1)}, u32[]{:S(2)}, u32[]{:S(2)}) collective-permute-start(f32[792,128]{1,0:T(8,128)} %get-tuple-element.546), channel_id=1, source_target_pairs={{0,32},{32,64},{64,96},{96,128},{128,160},{160,192},{192,224},{224... | collective-permute-start | bytes 1216520 | tf_op jit(solution)/shard_map/ppermute | solution.py:459
  8.0 0.0 collective-permute-start.9
  8.0 5.9 %collective-permute-start.13 = (f32[64,128]{1,0:T(8,128)}, f32[64,128]{1,0:T(8,128)S(1)}, u32[]{:S(2)}, u32[]{:S(2)}) collective-permute-start(f32[64,128]{1,0:T(8,128)} %get-tuple-element.550), channel_id=1, source_target_pairs={{0,31},{1,0},{2,1},{3,2},{4,3},{5,4},{6,5},{7,6},{8,7},{9,8},{10,9... | collective-permute-start | bytes 98312 | tf_op jit(solution)/shard_map/ppermute | solution.py:459
  13.8 0.0 collective-permute-done.12
  13.8 1.3 %collective-permute-done.13 = f32[64,128]{1,0:T(8,128)S(1)} collective-permute-done((f32[64,128]{1,0:T(8,128)}, f32[64,128]{1,0:T(8,128)S(1)}, u32[]{:S(2)}, u32[]{:S(2)}) %collective-permute-start.13) | collective-permute-done | bytes 32800 | tf_op jit(solution)/shard_map/ppermute | solution.py:459
  15.2 2.6 %collective-permute-start.14 = (f32[128,128]{1,0:T(8,128)S(1)}, f32[128,128]{1,0:T(8,128)S(1)}, u32[]{:S(2)}, u32[]{:S(2)}) collective-permute-start(f32[128,128]{1,0:T(8,128)S(1)} %constant_dynamic-update-slice_fusion.own_strip), channel_id=1, source_target_pairs={{0,32},{32,64},{64,96},{96,128},{128,160},{160,192},{192,224},{224... | collective-permute-start | bytes 196616 | tf_op jit(solution)/shard_map/ppermute | solution.py:459
  17.8 0.1 collective-permute-start.15
  17.9 1.2 %collective-permute-start.10 = (f32[264,128]{1,0:T(8,128)}, f32[264,128]{1,0:T(8,128)S(1)}, u32[]{:S(2)}, u32[]{:S(2)}) collective-permute-start(f32[264,128]{1,0:T(8,128)} %get-tuple-element.547), channel_id=1, source_target_pairs={{0,64},{32,96},{64,128},{96,160},{128,192},{160,224},{192,0},{224,... | collective-permute-start | bytes 405512 | tf_op jit(solution)/shard_map/ppermute | solution.py:459
  19.1 0.0 collective-permute-done.14.strip_b1
  19.1 2.6 %collective-permute-start.11 = (f32[264,128]{1,0:T(8,128)}, f32[264,128]{1,0:T(8,128)S(1)}, u32[]{:S(2)}, u32[]{:S(2)}) collective-permute-start(f32[264,128]{1,0:T(8,128)} %get-tuple-element.548), channel_id=1, source_target_pairs={{0,192},{32,224},{64,0},{96,32},{128,64},{160,96},{192,128},{224,1... | collective-permute-start | bytes 405512 | tf_op jit(solution)/shard_map/ppermute | solution.py:459
  21.7 0.1 collective-permute-done.15.strip_a1
  21.8 1.0 %collective-permute-start.16 = (f32[128,128]{1,0:T(8,128)S(1)}, f32[128,128]{1,0:T(8,128)S(1)}, u32[]{:S(2)}, u32[]{:S(2)}) collective-permute-start(f32[128,128]{1,0:T(8,128)S(1)} %constant_dynamic-update-slice_fusion.own_strip), channel_id=1, source_target_pairs={{0,64},{32,96},{64,128},{96,160},{128,192},{160,224},{192,0},{224,... | collective-permute-start | bytes 196616 | tf_op jit(solution)/shard_map/ppermute | solution.py:459
  22.8 4.4 %collective-permute-done.16.strip_b2 = f32[128,128]{1,0:T(8,128)S(1)} collective-permute-done((f32[128,128]{1,0:T(8,128)S(1)}, f32[128,128]{1,0:T(8,128)S(1)}, u32[]{:S(2)}, u32[]{:S(2)}) %collective-permute-start.16) | collective-permute-done | bytes 65568 | tf_op jit(solution)/shard_map/ppermute | solution.py:459
  27.2 1.5 %collective-permute-start.17 = (f32[128,128]{1,0:T(8,128)S(1)}, f32[128,128]{1,0:T(8,128)S(1)}, u32[]{:S(2)}, u32[]{:S(2)}) collective-permute-start(f32[128,128]{1,0:T(8,128)S(1)} %constant_dynamic-update-slice_fusion.own_strip), channel_id=1, source_target_pairs={{0,192},{32,224},{64,0},{96,32},{128,64},{160,96},{192,128},{224,1... | collective-permute-start | bytes 196616 | tf_op jit(solution)/shard_map/ppermute | solution.py:459
  28.7 1.6 %collective-permute-done.17.strip_a2 = f32[128,128]{1,0:T(8,128)S(1)} collective-permute-done((f32[128,128]{1,0:T(8,128)S(1)}, f32[128,128]{1,0:T(8,128)S(1)}, u32[]{:S(2)}, u32[]{:S(2)}) %collective-permute-start.17) | collective-permute-done | bytes 65568 | tf_op jit(solution)/shard_map/ppermute | solution.py:459
  30.4 0.0 collective-permute-done.10.below2
  30.4 0.0 collective-permute-done.11.above2
  30.4 0.0 copy-start.13
  30.4 0.0 collective-permute-done.8.below1
  30.4 0.0 copy-start.8
  30.4 0.0 collective-permute-done.9.above1
  30.4 0.0 copy-done.11
  30.4 0.0 copy-done.14
  30.4 0.0 copy-done.15
  30.5 0.5 copy-done.17
  31.0 0.1 copy-done.12
  31.0 0.1 copy-done.13
  31.1 0.1 copy-done.8
  31.2 0.8 %copy-done.9 = f32[792,128]{1,0:T(8,128)} copy-done((f32[792,128]{1,0:T(8,128)}, f32[792,128]{1,0:T(8,128)S(1)}, u32[]{:S(2)}) %copy-start.9) | copy-done | bytes 405528
  32.0 0.0 copy-done.10
  32.0 7.2 %shard_map.87 = (f32[6,64,512]{2,1,0:T(8,128)}, f32[1,128]{1,0:T(1,128)}) custom-call(f32[8,8]{1,0:T(8,128)S(1)} %copy-done.1, f32[8]{0:T(128)S(1)} %copy-done.3, f32[256,128]{1,0:T(8,128)} %bitcast.520, f32[256,128]{1,0:T(8,128)} %bitcast.518, f32[256,128]{1,0:T(8,128)} %bitcast.516, f32[4,128]{1,0:T(4,128)S(1)} %copy-done.2, s32[16,128]{1,0:T(8,128)S(1)} %bitcast.524, ...), custom_call_target="tpu_custom_call" | custom-call | tf_op jit(solution)/shard_map/pallas_call | solution.py:476
  39.2 0.7 copy-done.18
  39.9 0.7 broadcast_in_dim.114
  40.6 11.5 %all-to-all-start.4 = ((f32[256,1,128]{2,1,0:T(1,128)}), f32[256,1,128]{2,1,0:T(1,128)S(1)}, u32[]{:S(2)}, u32[]{:S(2)}) async-start(f32[256,1,128]{2,1,0:T(1,128)} %broadcast_in_dim.114), calls=%async_computation.4 | async-start | bytes 262144 | tf_op jit(solution)/shard_map/all_to_all | solution.py:496
  52.1 0.0 copy-start.5
  52.2 0.9 %copy-done.5 = f32[64,4,128]{2,1,0:T(4,128)S(1)} copy-done((f32[64,4,128]{2,1,0:T(4,128)S(1)}, f32[64,4,128]{2,1,0:T(4,128)}, u32[]{:S(2)}) %copy-start.5) | copy-done | bytes 131096
  53.1 0.9 %copy-done.6 = f32[64,4,128]{2,1,0:T(4,128)S(1)} copy-done((f32[64,4,128]{2,1,0:T(4,128)S(1)}, f32[64,4,128]{2,1,0:T(4,128)}, u32[]{:S(2)}) %copy-start.6) | copy-done | bytes 131096
  54.0 11.2 %all-to-all-done.4 = f32[256,1,128]{2,1,0:T(1,128)S(1)} async-done(((f32[256,1,128]{2,1,0:T(1,128)}), f32[256,1,128]{2,1,0:T(1,128)S(1)}, u32[]{:S(2)}, u32[]{:S(2)}) %all-to-all-start.4) | async-done | bytes 131104 | tf_op jit(solution)/shard_map/all_to_all | solution.py:496
  65.2 0.7 copy-done.7
  65.8 2.5 %shard_map.88 = (f32[6,256,128]{2,1,0:T(8,128)}, f32[6,5]{1,0:T(8,128)}, f32[1,128]{1,0:T(1,128)}) custom-call(f32[8,8]{1,0:T(8,128)S(1)} %copy-done.1, f32[8]{0:T(128)S(1)} %copy-done.3, f32[6,64,512]{2,1,0:T(8,128)} %get-tuple-element.551.powers, f32[256,128]{1,0:T(8,128)} %bitcast.522), custom_call_target="tpu_custom_call" | custom-call | tf_op jit(solution)/shard_map/pallas_call | solution.py:497
  68.3 2.1 %copy.140 = f32[6,64,4,128]{3,1,2,0:T(8,128)} copy(f32[6,64,4,128]{3,2,1,0:T(4,128)} %bitcast.521) | data formatting | bytes 1572864 | tf_op jit(solution)/shard_map/while | solution.py:517
  70.4 0.7 copy-done.19
  71.2 0.2 while.39
  71.3 2.5 %copy.144 = f32[6,64,4,128]{3,2,1,0:T(4,128)} copy(f32[6,64,4,128]{3,1,2,0:T(8,128)} %get-tuple-element.1023) | data formatting | bytes 1572864
  (24 shorter events, 0.1 us)
Async XLA Ops:
  0.6 0.7 copy-start.2
  3.4 10.5 %collective-permute-start.12 = (f32[64,128]{1,0:T(8,128)}, f32[64,128]{1,0:T(8,128)S(1)}, u32[]{:S(2)}, u32[]{:S(2)}) collective-permute-start(f32[64,128]{1,0:T(8,128)} %get-tuple-element.549), channel_id=1, source_target_pairs={{0,1},{1,2},{2,3},{3,4},{4,5},{5,6},{6,7},{7,8},{8,9},{9,10},{10,1... | collective-permute-start | bytes 98312 | tf_op jit(solution)/shard_map/ppermute | solution.py:459
  5.8 24.5 %collective-permute-start.8 = (f32[792,128]{1,0:T(8,128)}, f32[792,128]{1,0:T(8,128)S(1)}, u32[]{:S(2)}, u32[]{:S(2)}) collective-permute-start(f32[792,128]{1,0:T(8,128)} %get-tuple-element.546), channel_id=1, source_target_pairs={{0,32},{32,64},{64,96},{96,128},{128,160},{160,192},{192,224},{224... | collective-permute-start | bytes 1216520 | tf_op jit(solution)/shard_map/ppermute | solution.py:459
  8.0 22.4 %collective-permute-start.9 = (f32[792,128]{1,0:T(8,128)}, f32[792,128]{1,0:T(8,128)S(1)}, u32[]{:S(2)}, u32[]{:S(2)}) collective-permute-start(f32[792,128]{1,0:T(8,128)} %get-tuple-element.546), channel_id=1, source_target_pairs={{0,224},{32,0},{64,32},{96,64},{128,96},{160,128},{192,160},{224,1... | collective-permute-start | bytes 1216520 | tf_op jit(solution)/shard_map/ppermute | solution.py:459
  8.0 7.2 %collective-permute-start.13 = (f32[64,128]{1,0:T(8,128)}, f32[64,128]{1,0:T(8,128)S(1)}, u32[]{:S(2)}, u32[]{:S(2)}) collective-permute-start(f32[64,128]{1,0:T(8,128)} %get-tuple-element.550), channel_id=1, source_target_pairs={{0,31},{1,0},{2,1},{3,2},{4,3},{5,4},{6,5},{7,6},{8,7},{9,8},{10,9... | collective-permute-start | bytes 98312 | tf_op jit(solution)/shard_map/ppermute | solution.py:459
  15.2 16.8 %copy-start.1 = (f32[8,8]{1,0:T(8,128)S(1)}, f32[8,8]{1,0:T(8,128)}, u32[]{:S(2)}) copy-start(f32[8,8]{1,0:T(8,128)} %line_ref.3) | copy-start | bytes 772
  15.2 16.8 %copy-start.10 = (s32[4,4,128]{2,1,0:T(4,128)S(1)}, s32[4,4,128]{2,1,0:T(4,128)}, u32[]{:S(2)}) copy-start(s32[4,4,128]{2,1,0:T(4,128)} %param.35) | copy-start | bytes 24580
  15.2 15.2 %copy-start.11 = (f32[128,128]{1,0:T(8,128)}, f32[128,128]{1,0:T(8,128)S(1)}, u32[]{:S(2)}) copy-start(f32[128,128]{1,0:T(8,128)S(1)} %constant_dynamic-update-slice_fusion.own_strip) | copy-start | bytes 196612
  15.2 3.9 %collective-permute-start.14 = (f32[128,128]{1,0:T(8,128)S(1)}, f32[128,128]{1,0:T(8,128)S(1)}, u32[]{:S(2)}, u32[]{:S(2)}) collective-permute-start(f32[128,128]{1,0:T(8,128)S(1)} %constant_dynamic-update-slice_fusion.own_strip), channel_id=1, source_target_pairs={{0,32},{32,64},{64,96},{96,128},{128,160},{160,192},{192,224},{224... | collective-permute-start | bytes 196616 | tf_op jit(solution)/shard_map/ppermute | solution.py:459
  17.8 4.0 %collective-permute-start.15 = (f32[128,128]{1,0:T(8,128)S(1)}, f32[128,128]{1,0:T(8,128)S(1)}, u32[]{:S(2)}, u32[]{:S(2)}) collective-permute-start(f32[128,128]{1,0:T(8,128)S(1)} %constant_dynamic-update-slice_fusion.own_strip), channel_id=1, source_target_pairs={{0,224},{32,0},{64,32},{96,64},{128,96},{160,128},{192,160},{224,1... | collective-permute-start | bytes 196616 | tf_op jit(solution)/shard_map/ppermute | solution.py:459
  17.9 14.1 %copy-start.3 = (f32[8]{0:T(128)S(1)}, f32[8]{0:T(128)}, u32[]{:S(2)}) copy-start(f32[8]{0:T(128)} %deriv_ref.3) | copy-start | bytes 100
  17.9 12.5 %collective-permute-start.10 = (f32[264,128]{1,0:T(8,128)}, f32[264,128]{1,0:T(8,128)S(1)}, u32[]{:S(2)}, u32[]{:S(2)}) collective-permute-start(f32[264,128]{1,0:T(8,128)} %get-tuple-element.547), channel_id=1, source_target_pairs={{0,64},{32,96},{64,128},{96,160},{128,192},{160,224},{192,0},{224,... | collective-permute-start | bytes 405512 | tf_op jit(solution)/shard_map/ppermute | solution.py:459
  19.1 11.3 %copy-start.14 = (f32[128,128]{1,0:T(8,128)}, f32[128,128]{1,0:T(8,128)S(1)}, u32[]{:S(2)}) copy-start(f32[128,128]{1,0:T(8,128)S(1)} %collective-permute-done.14.strip_b1) | copy-start | bytes 196612
  19.1 11.2 %collective-permute-start.11 = (f32[264,128]{1,0:T(8,128)}, f32[264,128]{1,0:T(8,128)S(1)}, u32[]{:S(2)}, u32[]{:S(2)}) collective-permute-start(f32[264,128]{1,0:T(8,128)} %get-tuple-element.548), channel_id=1, source_target_pairs={{0,192},{32,224},{64,0},{96,32},{128,64},{160,96},{192,128},{224,1... | collective-permute-start | bytes 405512 | tf_op jit(solution)/shard_map/ppermute | solution.py:459
  21.8 8.6 %copy-start.15 = (f32[128,128]{1,0:T(8,128)}, f32[128,128]{1,0:T(8,128)S(1)}, u32[]{:S(2)}) copy-start(f32[128,128]{1,0:T(8,128)S(1)} %collective-permute-done.15.strip_a1) | copy-start | bytes 196612
  21.8 5.4 %collective-permute-start.16 = (f32[128,128]{1,0:T(8,128)S(1)}, f32[128,128]{1,0:T(8,128)S(1)}, u32[]{:S(2)}, u32[]{:S(2)}) collective-permute-start(f32[128,128]{1,0:T(8,128)S(1)} %constant_dynamic-update-slice_fusion.own_strip), channel_id=1, source_target_pairs={{0,64},{32,96},{64,128},{96,160},{128,192},{160,224},{192,0},{224,... | collective-permute-start | bytes 196616 | tf_op jit(solution)/shard_map/ppermute | solution.py:459
  27.2 3.2 %copy-start.16 = (f32[128,128]{1,0:T(8,128)}, f32[128,128]{1,0:T(8,128)S(1)}, u32[]{:S(2)}) copy-start(f32[128,128]{1,0:T(8,128)S(1)} %collective-permute-done.16.strip_b2) | copy-start | bytes 196612
  27.2 3.1 %collective-permute-start.17 = (f32[128,128]{1,0:T(8,128)S(1)}, f32[128,128]{1,0:T(8,128)S(1)}, u32[]{:S(2)}, u32[]{:S(2)}) collective-permute-start(f32[128,128]{1,0:T(8,128)S(1)} %constant_dynamic-update-slice_fusion.own_strip), channel_id=1, source_target_pairs={{0,192},{32,224},{64,0},{96,32},{128,64},{160,96},{192,128},{224,1... | collective-permute-start | bytes 196616 | tf_op jit(solution)/shard_map/ppermute | solution.py:459
  30.4 0.6 copy-start.17
  30.4 0.7 copy-start.12
  30.4 0.7 copy-start.13
  30.4 0.8 %copy-start.8 = (f32[792,128]{1,0:T(8,128)}, f32[792,128]{1,0:T(8,128)S(1)}, u32[]{:S(2)}) copy-start(f32[792,128]{1,0:T(8,128)S(1)} %collective-permute-done.8.below1) | copy-start | bytes 1216516
  31.2 0.8 %copy-start.9 = (f32[792,128]{1,0:T(8,128)}, f32[792,128]{1,0:T(8,128)S(1)}, u32[]{:S(2)}) copy-start(f32[792,128]{1,0:T(8,128)S(1)} %collective-permute-done.9.above1) | copy-start | bytes 1216516
  39.2 0.7 copy-start.18
  40.6 11.6 %copy-start.4 = (f32[64,4,128]{2,1,0:T(4,128)S(1)}, f32[64,4,128]{2,1,0:T(4,128)}, u32[]{:S(2)}) copy-start(f32[64,4,128]{2,1,0:T(4,128)} %param.31) | copy-start | bytes 393220
  40.6 24.6 %all-to-all-start.4 = ((f32[256,1,128]{2,1,0:T(1,128)}), f32[256,1,128]{2,1,0:T(1,128)S(1)}, u32[]{:S(2)}, u32[]{:S(2)}) async-start(f32[256,1,128]{2,1,0:T(1,128)} %broadcast_in_dim.114), calls=%async_computation.4 | async-start | bytes 262144 | tf_op jit(solution)/shard_map/all_to_all | solution.py:496
  52.1 0.9 %copy-start.5 = (f32[64,4,128]{2,1,0:T(4,128)S(1)}, f32[64,4,128]{2,1,0:T(4,128)}, u32[]{:S(2)}) copy-start(f32[64,4,128]{2,1,0:T(4,128)} %param.30) | copy-start | bytes 393220
  53.0 0.9 %copy-start.6 = (f32[64,4,128]{2,1,0:T(4,128)S(1)}, f32[64,4,128]{2,1,0:T(4,128)}, u32[]{:S(2)}) copy-start(f32[64,4,128]{2,1,0:T(4,128)} %param.29) | copy-start | bytes 393220
  65.2 0.7 copy-start.7
  70.4 0.7 copy-start.19
